TPU v7x, 32 devices: a whole 2x2x4 slice. The times are simulated.
32 devices in a mesh: ep: 8 (over z, x), corner: 4 (over y, core).
Axes of the slice: x: 2, y: 2, z: 4, core: 2. Of those that a mesh axis runs over, the one named last changes fastest.
Arguments:
- required: float32 [8, 262144], P('corner', 'ep'), may hold values from -3 to 3
- arrival: float32 [8, 262144], P('corner', 'ep'), may hold values from -7.2 to 7.2
- hold_required: float32 [8, 262144], P('corner', 'ep'), may hold values from -5.4 to 5.4
- early_arrival: float32 [8, 262144], P('corner', 'ep'), may hold values from -3 to 3
- part_ids: int32 [262144], P('ep'), may hold values from 0 to 63
- bin_edges: int32 [512], replicated, may hold values from -4096 to -1, as said below
Outputs:
- part_hist: float32 [64, 8, 2, 512], P(None, 'corner')
- part_tns: float32 [64, 8, 2], P(None, 'corner')
- part_share: float32 [64], replicated
- tns: float32 [8, 2], P('corner')
- wns: float32 [8, 2], P('corner')
- worst: float32 [2, 262144], P(None, 'ep')
Inputs may be any that keep to these rules, and one draw needn't show every extreme that they name: `bin_edges`: strictly increasing and negative; consecutive nodes differ by 1 to 8.
All inputs are finite; a program needn't handle non-finite values.
Results may differ from a plain program's by a relative error of at most 0.0003.
Values sent between devices are 32-bit elements; how exact they have to be, the bound alone decides.
A program may use at most 64 MiB of HBM per device.

v0:
```python
import functools
import jax
import jax.numpy as jnp
from jax import lax
from jax.experimental import pallas as pl
from jax.experimental.pallas import tpu as pltpu
from jax.sharding import PartitionSpec as P

GROUPS = 64
HIGH = 4
LANES = 128
EXTRA = 16
HALF = 1024
DEPTH = 4096
MESH = pl.DeviceIdType.MESH


def pick(table, index):
    return jnp.take_along_axis(table, index, axis=1, mode="promise_in_bounds")


def make_tables(edges_ref):
    nodes = edges_ref[...].astype(jnp.float32) * 0.001
    lane = lax.broadcasted_iota(jnp.int32, (8, LANES), 1)
    rows = [jnp.broadcast_to(nodes[q : q + 1], (8, LANES)) for q in range(4)]
    third = []
    for j in range(8):
        index = (8 * lane + j) & 127
        parts = [pick(row, index) for row in rows]
        value = parts[3]
        for q in (2, 1, 0):
            value = jnp.where(lane < 16 * (q + 1), parts[q], value)
        third.append(value)
    following = pick(third[0], jnp.minimum(lane + 1, LANES - 1))
    third.append(jnp.where(lane >= 63, 0.0, following))
    second = [pick(third[0], (8 * lane + j) & 63) for j in range(1, 8)]
    first = [pick(third[0], jnp.full((8, LANES), 8 * i, jnp.int32)) for i in range(1, 8)]
    lowest = pick(third[0], jnp.zeros((8, LANES), jnp.int32))
    return first, second, third, lowest


def search(tables, slack):
    first, second, third, lowest = tables
    level = jnp.minimum(jnp.maximum(slack, lowest), 0.0)
    group = jnp.zeros(level.shape, jnp.int32)
    for bound in first:
        group += (level >= bound).astype(jnp.int32)
    finer = group * 8
    for table in second:
        finer += (level >= pick(table, group)).astype(jnp.int32)
    index = finer * 8
    low = pick(third[0], finer)
    high = pick(third[8], finer)
    inner = [pick(table, finer) for table in third[1:8]]
    for value in inner:
        above = level >= value
        index += above.astype(jnp.int32)
        low = jnp.where(above, value, low)
    for value in reversed(inner):
        high = jnp.where(level < value, value, high)
    scale = 1.0 / (high - low)
    return index, (high - level) * scale, (level - low) * scale


def search_kernel(req, arr, hreq, early, ids, edges, marks_out, worst_out, least_out):
    corners, rows = req.shape
    combos = 2 * corners
    halves = 8 // combos
    depth = halves * HALF
    tables = make_tables(edges)

    def block(step, smallest):
        slabs, parts, spans = [], [], []
        for half in range(halves):
            at = pl.ds(pl.multiple_of(step * depth + half * HALF, HALF), HALF)
            setup = req[:, at] - arr[:, at]
            hold = early[:, at] - hreq[:, at]
            worst_out[0:1, at] = jnp.min(setup, axis=0, keepdims=True)
            worst_out[1:2, at] = jnp.min(hold, axis=0, keepdims=True)
            slabs += [setup, hold]
            parts.append(jnp.broadcast_to(ids[:, at], (combos, HALF)))
            spans.append(at)
        slab = jnp.concatenate(slabs, axis=0)
        part = jnp.concatenate(parts, axis=0)
        low_at, code, w_first, w_second = [], [], [], []
        for lane in range(0, HALF, LANES):
            piece = slab[:, lane : lane + LANES]
            smallest = jnp.minimum(smallest, piece)
            index, wa, wb = search(tables, piece)
            low_at.append((index & (LANES - 1)).astype(jnp.float32))
            code.append(((index >> 7) * GROUPS + part[:, lane : lane + LANES]).astype(jnp.float32))
            w_first.append(wa)
            w_second.append(wb)
        marks = [jnp.concatenate(v, axis=1) for v in (low_at, code, w_first, w_second)]
        marks.append(jnp.minimum(slab, 0.0))
        for q, v in enumerate(marks):
            for half in range(halves):
                marks_out[q, :, spans[half]] = v[half * combos : (half + 1) * combos]
        return smallest

    start = jnp.full((8, LANES), jnp.inf, jnp.float32)
    smallest = lax.fori_loop(0, rows // depth, block, start)
    least_out[...] = jnp.broadcast_to(jnp.min(smallest, axis=1, keepdims=True), (8, LANES))


def report_kernel(
    n, nc, density,
    marks, worst, least, hist_out, stats_out, worst_out,
    acc, hist, hist_in, stats, stats_in, worst_in,
    hs, hr, gs, gr, ss, sr, ws, wr, vs, vr,
):
    combos, rows = marks.shape[1:]
    me = lax.axis_index("ep")
    mc = lax.axis_index("corner")
    chunk = GROUPS // n
    width = worst.shape[1] // nc
    narrow = jnp.bfloat16
    barrier = pltpu.get_barrier_semaphore()
    for d in range(1, n):
        pl.semaphore_signal(
            barrier, inc=1, device_id={"ep": lax.rem(me + d, n)}, device_id_type=MESH
        )
    for d in range(1, nc):
        pl.semaphore_signal(
            barrier, inc=1, device_id={"corner": lax.rem(mc + d, nc)}, device_id_type=MESH
        )
    pl.semaphore_wait(barrier, n - 1 + nc - 1)

    def send(src, dst, s_sem, r_sem, target):
        copy = pltpu.make_async_remote_copy(
            src_ref=src, dst_ref=dst, send_sem=s_sem, recv_sem=r_sem,
            device_id=target, device_id_type=MESH,
        )
        copy.start()
        return copy

    def lanes(k):
        return pl.ds(pl.multiple_of(k * width, LANES), width)

    mins = []
    for d in range(1, nc):
        t = lax.rem(mc + d, nc)
        mins.append(
            send(worst.at[:, lanes(t)], worst_in.at[d], ws.at[d], wr.at[d], {"corner": t})
        )

    iota_low = lax.broadcasted_iota(jnp.int32, (16, DEPTH), 0).astype(jnp.float32).astype(narrow)
    zero = jnp.zeros((16, DEPTH), narrow)
    one = jnp.ones((16, DEPTH), narrow)

    def product(r, first, last):
        def block(step, carry):
            at = pl.ds(pl.multiple_of(step * DEPTH, DEPTH), DEPTH)

            def row(q):
                return marks[q, r : r + 1, at]

            def spread(v):
                return jnp.broadcast_to(v, (16, DEPTH)).astype(narrow)

            at_low, at_code, wa, wb = (spread(row(q)) for q in range(4))
            neg = row(4)
            piece_a = neg.astype(narrow).astype(jnp.float32)
            rest = neg - piece_a
            piece_b = rest.astype(narrow).astype(jnp.float32)
            piece_c = rest - piece_b
            left = []
            for start in range(0, LANES, 16):
                left.append(
                    jnp.where(
                        at_low == iota_low + narrow(start),
                        wa,
                        jnp.where(at_low == iota_low + narrow(start - 1), wb, zero),
                    )
                )
            tail = jnp.where(at_low == narrow(LANES - 1), wb, zero)
            tail = jnp.where(iota_low == narrow(0), tail, zero)
            for place, v in ((1, piece_a), (2, piece_b), (3, piece_c)):
                tail = jnp.where(iota_low == narrow(place), spread(v), tail)
            left.append(jnp.where(iota_low == narrow(4), one, tail))
            right = [
                jnp.where(at_code == iota_low + narrow(start), one, zero)
                for start in range(0, HIGH * GROUPS, 16)
            ]
            acc[...] += lax.dot_general(
                jnp.concatenate(left, axis=0),
                jnp.concatenate(right, axis=0),
                (((1,), (1,)), ((), ())),
                preferred_element_type=jnp.float32,
            )
            return carry

        lax.fori_loop(first, last, block, 0)

    lane = lax.broadcasted_iota(jnp.int32, (1, HIGH * GROUPS), 1)

    def fold(v):
        v = v[:, :LANES] + v[:, LANES:]
        return v + pltpu.roll(jnp.broadcast_to(v, (8, LANES)), GROUPS, 1)[0:1]

    def settle(r):
        full = acc[...]
        over = jnp.broadcast_to(full[LANES : LANES + 1], (8, HIGH * GROUPS))
        over = pltpu.roll(over, GROUPS, 1)[0:1]
        acc[0:1] = full[0:1] + jnp.where(lane >= GROUPS, over, 0.0)
        turned = acc[0:LANES].T
        for k in range(n):
            for g in range(HIGH):
                top = g * GROUPS + k * chunk
                hist[r, k, :, g * LANES : (g + 1) * LANES] = turned[top : top + chunk]
        pieces = [full[LANES + 1 + i : LANES + 2 + i] for i in range(3)]
        stats[r : r + 1] = fold(pieces[0] + pieces[1] + pieces[2])
        if r == 0:
            stats[combos : combos + 1] = fold(full[LANES + 4 : LANES + 5])

    def scatter(r):
        copies = []
        for d in range(1, n):
            t = lax.rem(me + d, n)
            copies.append(
                send(hist.at[r, t], hist_in.at[r, d], hs.at[r, d], hr.at[r, d], {"ep": t})
            )
        return copies

    def gather(r, scattered):
        total = hist[r, me]
        for d in range(1, n):
            scattered[d - 1].wait_recv()
            total += hist_in[r, d]
        hist_out[r, me] = total * density
        copies = []
        for d in range(1, n):
            t = lax.rem(me + d, n)
            part = hist_out.at[r, me]
            copies.append(send(part, part, gs.at[r, d], gr.at[r, d], {"ep": t}))
        return copies

    steps = rows // DEPTH
    stats[...] = jnp.zeros_like(stats)
    stats[8:16] = least[...]
    sent, spread_out, gathered = [], [], []
    for r in range(combos):
        acc[...] = jnp.zeros_like(acc)
        product(r, 0, steps // 2)
        if r == 0:
            for copy in mins:
                copy.wait_recv()
            low = worst[:, lanes(mc)]
            for d in range(1, nc):
                low = jnp.minimum(low, worst_in[d])
            worst_out[:, lanes(mc)] = low
            for d in range(1, nc):
                t = lax.rem(mc + d, nc)
                part = worst_out.at[:, lanes(mc)]
                spread_out.append(send(part, part, vs.at[d], vr.at[d], {"corner": t}))
        else:
            gathered += gather(r - 1, sent[-1])
        product(r, steps // 2, steps)
        settle(r)
        sent.append(scatter(r))
    shares = []
    for d in range(1, n):
        t = lax.rem(me + d, n)
        shares.append(send(stats, stats_in.at[me], ss.at[d], sr.at[d], {"ep": t}))
    gathered += gather(combos - 1, sent[-1])
    for copy in shares:
        copy.wait_recv()
    stats_in[me] = stats[...]
    added = stats_in[0, 0:8]
    lowest = stats_in[0, 8:16]
    for k in range(1, n):
        added += stats_in[k, 0:8]
        lowest = jnp.minimum(lowest, stats_in[k, 8:16])
    stats_out[0:8] = added
    stats_out[8:16] = lowest
    for copy in spread_out + gathered:
        copy.wait_recv()
    for copy in mins + sum(sent, []) + shares + spread_out + gathered:
        copy.wait_send()


def finish_kernel(endpoints, hist, stats, worst, hist_out, tns_out, share_out, total_out, least_out, worst_out):
    corners = total_out.shape[0]
    combos = 2 * corners
    share = GROUPS / endpoints
    for m in range(2):
        for c in range(corners):
            r = m * corners + c
            hist_out[:, c, m, :] = hist[r]
            row = stats[r : r + 1, :GROUPS]
            tns_out[c, m : m + 1, :] = row * share
            total = jnp.sum(row, axis=1, keepdims=True) * (1.0 / endpoints)
            total_out[c : c + 1, m : m + 1] = total
            low = stats[8 + r : 9 + r, 0:1]
            for top in range(8 + combos, 16, combos):
                low = jnp.minimum(low, stats[top + r : top + r + 1, 0:1])
            least_out[c : c + 1, m : m + 1] = low
    share_out[...] = stats[combos : combos + 1, :GROUPS] * share
    worst_out[...] = worst[...]


def on_device(required, arrival, hold_required, early_arrival, part_ids, bin_edges):
    corners, rows = required.shape
    n, nc = lax.axis_size("ep"), lax.axis_size("corner")
    endpoints = rows * n
    bins = bin_edges.shape[0]
    combos = 2 * corners
    f32 = jnp.float32
    vmem = pl.BlockSpec(memory_space=pltpu.VMEM)
    marks, worst, least = pl.pallas_call(
        search_kernel,
        out_shape=(
            jax.ShapeDtypeStruct((5, combos, rows), f32),
            jax.ShapeDtypeStruct((2, rows), f32),
            jax.ShapeDtypeStruct((8, LANES), f32),
        ),
        in_specs=[vmem] * 6,
        out_specs=[vmem] * 3,
        name="node_search",
    )(
        required, arrival, hold_required, early_arrival,
        part_ids.reshape(1, rows), bin_edges.reshape(bins // LANES, LANES),
    )
    dma = pltpu.SemaphoreType.DMA
    blocks = (combos, n, GROUPS // n, bins)
    hist, stats, worst = pl.pallas_call(
        functools.partial(report_kernel, n, nc, GROUPS * bins / endpoints),
        out_shape=(
            jax.ShapeDtypeStruct(blocks, f32),
            jax.ShapeDtypeStruct((16, LANES), f32),
            jax.ShapeDtypeStruct((2, rows), f32),
        ),
        in_specs=[vmem] * 3,
        out_specs=[vmem] * 3,
        scratch_shapes=[
            pltpu.VMEM((LANES + EXTRA, HIGH * GROUPS), f32),
            pltpu.VMEM(blocks, f32),
            pltpu.VMEM(blocks, f32),
            pltpu.VMEM((16, LANES), f32),
            pltpu.VMEM((n, 16, LANES), f32),
            pltpu.VMEM((nc, 2, rows // nc), f32),
        ]
        + [dma((combos, n))] * 4
        + [dma((n,))] * 2
        + [dma((nc,))] * 4,
        compiler_params=pltpu.CompilerParams(collective_id=0, has_side_effects=True),
        name="report",
    )(marks, worst, least)
    part_hist, part_tns, part_share, tns, wns, worst = pl.pallas_call(
        functools.partial(finish_kernel, endpoints),
        out_shape=(
            jax.ShapeDtypeStruct((GROUPS, corners, 2, bins), f32),
            jax.ShapeDtypeStruct((corners, 2, GROUPS), f32),
            jax.ShapeDtypeStruct((1, GROUPS), f32),
            jax.ShapeDtypeStruct((corners, 2), f32),
            jax.ShapeDtypeStruct((corners, 2), f32),
            jax.ShapeDtypeStruct((2, rows), f32),
        ),
        in_specs=[vmem] * 3,
        out_specs=[vmem] * 6,
        name="finish",
    )(hist.reshape(combos, GROUPS, bins), stats, worst)
    return (part_hist, part_tns.transpose(2, 0, 1), part_share[0], tns, wns, worst)


def solution(mesh):
    in_specs = (
        P("corner", "ep"),
        P("corner", "ep"),
        P("corner", "ep"),
        P("corner", "ep"),
        P("ep"),
        P(),
    )
    out_specs = (
        P(None, "corner", None, None),
        P(None, "corner", None),
        P(),
        P("corner", None),
        P("corner", None),
        P(None, "ep"),
    )
    return jax.shard_map(
        on_device, mesh=mesh, in_specs=in_specs, out_specs=out_specs, check_vma=False
    )
```

profile of v0, /device:TPU:0, one launch (start us, length us, event | category | flops | bytes accessed | tf_op | source)
XLA Modules:
  0.0 64.9 jit_solution(13851009084064597722)
XLA Ops:
  0.6 10.1 %node_search.1 = (f32[5,4,32768]{2,1,0:T(4,128)}, f32[2,32768]{1,0:T(2,128)}, f32[8,128]{1,0:T(8,128)}) custom-call(f32[2,32768]{1,0:T(2,128)} %req.1, f32[2,32768]{1,0:T(2,128)} %arr.1, f32[2,32768]{1,0:T(2,128)} %hreq.1, f32[2,32768]{1,0:T(2,128)} %early.1, s32[1,32768]{1,0:T(1,128)} %bitcast.6, s32[4,128]{1,0:T(4,128)} %bitcast.7), custom_call_target="tpu_custom_call" | custom-call | tf_op jit(solution)/shard_map/node_search/pallas_call | solution.py:310
  10.8 52.0 %report.1 = (f32[4,8,8,512]{3,2,1,0:T(8,128)}, f32[16,128]{1,0:T(8,128)}, f32[2,32768]{1,0:T(2,128)}) custom-call(f32[5,4,32768]{2,1,0:T(4,128)} %get-tuple-element.18.marks, f32[2,32768]{1,0:T(2,128)} %get-tuple-element.19.worst, f32[8,128]{1,0:T(8,128)} %get-tuple-element.20.least), custom_call_target="tpu_custom_call" | custom-call | tf_op jit(solution)/shard_map/report/pallas_call | solution.py:326
  62.8 2.1 %finish.1 = (f32[64,2,2,512]{3,2,1,0:T(2,128)}, f32[2,2,64]{2,1,0:T(2,128)}, f32[1,64]{1,0:T(1,128)}, f32[2,2]{1,0:T(2,128)}, f32[2,2]{1,0:T(2,128)}, /*index=5*/f32[2,32768]{1,0:T(2,128)}) custom-call(f32[4,64,512]{2,1,0:T(8,128)} %bitcast.5, f32[16,128]{1,0:T(8,128)} %get-tuple-element.22.stats, f32[2,32768]{1,0:T(2,128)} %get-tuple-element.23.worst), custom_call_target="tpu_custom_call" | custom-call | tf_op jit(solution)/shard_map/finish/pallas_call | solution.py:349
where the time goes:
time: 65.1 us; the launch traced here: 64.9 us
  Pallas kernels  64.2 us (99%)
    pallas_call x1, Pallas kernels, on_device(): pl.pallas_call(functools.partial(report_kernel, n, nc, GROUPS * bins / en...  52 us
    pallas_call x1, Pallas kernels, on_device(): pl.pallas_call(search_kernel, out_shape=(jax.ShapeDtypeStruct((5, combos,...  10.1 us
    pallas_call x1, Pallas kernels, on_device(): pl.pallas_call(functools.partial(finish_kernel, endpoints), out_shape=(ja...  2.11 us

commit v1 on v0

v1 whole, which is shorter than its diff:
```python
import functools
import jax
import jax.numpy as jnp
from jax import lax
from jax.experimental import pallas as pl
from jax.experimental.pallas import tpu as pltpu
from jax.sharding import PartitionSpec as P

GROUPS = 64
LANES = 128
SUBS = 8
PACK = 16
PAIR = 2
FIELDS = 4
MESH = pl.DeviceIdType.MESH


def pick(table, index):
    return jnp.take_along_axis(table, index, axis=1, mode="promise_in_bounds")


def make_tables(edges_ref):
    nodes = edges_ref[...].astype(jnp.float32) * 0.001
    lane = lax.broadcasted_iota(jnp.int32, (SUBS, LANES), 1)
    rows = [jnp.broadcast_to(nodes[q : q + 1], (SUBS, LANES)) for q in range(4)]

    def gathered(place):
        index = place & (LANES - 1)
        value = pick(rows[3], index)
        for q in (2, 1, 0):
            value = jnp.where(place < LANES * (q + 1), pick(rows[q], index), value)
        return value

    def same(row):
        return pick(row, jnp.zeros((SUBS, LANES), jnp.int32))

    steps = []
    for k in range(2, 8):
        steps.append(gathered(((lane << (9 - k)) + (1 << (8 - k))) & 511))
    last = [gathered(2 * lane + 1), gathered(2 * lane + 2 * LANES + 1)]
    return [same(row) for row in rows], steps, last


def search(tables, slack):
    quarter, steps, last = tables
    level = jnp.minimum(jnp.maximum(slack, quarter[0]), 0.0)
    top = level >= quarter[2]
    low = jnp.where(top, quarter[2], quarter[0])
    high = jnp.where(top, 0.0, quarter[2])
    value = jnp.where(top, quarter[3], quarter[1])
    above = level >= value
    low = jnp.where(above, value, low)
    high = jnp.where(above, high, value)
    index = jnp.where(top, 2, 0) + jnp.where(above, 1, 0)
    part = index
    for table in steps:
        value = pick(table, index)
        above = level >= value
        low = jnp.where(above, value, low)
        high = jnp.where(above, high, value)
        index = index + index
        index = jnp.where(above, index + 1, index)
    place = index & (LANES - 1)
    value = jnp.where(top, pick(last[1], place), pick(last[0], place))
    above = level >= value
    low = jnp.where(above, value, low)
    high = jnp.where(above, high, value)
    scale = 1.0 / (high - low)
    first = (high - level) * scale
    second = (level - low) * scale
    odd_at = index & 63
    even_at = jnp.where(above, odd_at + 1, odd_at)
    even = jnp.where(above, second, first)
    odd = jnp.where(above, first, second)
    return part, even_at, odd_at, even, odd


def report_kernel(
    n, nc, density, plan,
    req, arr, hreq, early, ids, edges,
    hist_out, stats_out, worst_out,
    marks, codes, tail, acc, worst, worst_in, least,
    hist, pair_in, line_in, all_in, stats, stats_in,
    ps, pr, ls, lr, gs, gr, fs, fr, ss, sr, ws, wr, vs, vr,
):
    corners = hist.shape[0] // 2
    combos = 2 * corners
    blocks = ids.shape[0]
    steps = blocks // SUBS
    depth = steps * LANES
    chunk = GROUPS // n
    line = n // PAIR
    share = worst_out.shape[0] // nc
    narrow = jnp.bfloat16
    f32 = jnp.float32
    me = lax.axis_index("ep")
    mc = lax.axis_index("corner")
    mx = lax.rem(me, PAIR)
    mz = me // PAIR
    other = PAIR - 1 - mx
    mine = mx * line + mz

    barrier = pltpu.get_barrier_semaphore()
    for d in range(1, n):
        pl.semaphore_signal(
            barrier, inc=1, device_id={"ep": lax.rem(me + d, n)}, device_id_type=MESH
        )
    for d in range(1, nc):
        pl.semaphore_signal(
            barrier, inc=1, device_id={"corner": lax.rem(mc + d, nc)}, device_id_type=MESH
        )

    def send(src, dst, s_sem, r_sem, target):
        copy = pltpu.make_async_remote_copy(
            src_ref=src, dst_ref=dst, send_sem=s_sem, recv_sem=r_sem,
            device_id=target, device_id_type=MESH,
        )
        copy.start()
        return copy

    tables = make_tables(edges)
    sources = ((req, arr), (early, hreq))

    def smallest(step, carry):
        for kind, (plus, minus) in enumerate(sources):
            low = None
            for c in range(corners):
                at = pl.ds(corners * SUBS * step + c, SUBS, stride=corners)
                slack = plus[at, :] - minus[at, :]
                low = slack if low is None else jnp.minimum(low, slack)
            worst[pl.ds(2 * SUBS * step + kind, SUBS, stride=2), :] = low
        return carry

    lax.fori_loop(0, steps, smallest, 0, unroll=4)
    pl.semaphore_wait(barrier, n - 1 + nc - 1)

    def rows_of(k):
        return pl.ds(pl.multiple_of(k * share, SUBS), share)

    mins = []
    for d in range(1, nc):
        t = lax.rem(mc + d, nc)
        mins.append(send(worst.at[rows_of(t)], worst_in.at[d], ws.at[d], wr.at[d], {"corner": t}))

    def find(r):
        kind, c = r // corners, r % corners
        plus, minus = sources[kind]

        def body(step, low):
            at = pl.ds(corners * step + c, SUBS, stride=corners * steps)
            lanes = pl.ds(pl.multiple_of(step * LANES, LANES), LANES)
            slack = plus[at, :] - minus[at, :]
            part, even_at, odd_at, even, odd = search(tables, slack)
            group = ids[pl.ds(step, SUBS, stride=steps), :]
            codes[pl.ds(step, SUBS, stride=steps), :] = (part * GROUPS + group).astype(f32)
            for q, v in enumerate((even_at, odd_at)):
                marks[q, :, lanes] = v.astype(f32)
            marks[2, :, lanes] = even
            marks[3, :, lanes] = odd
            negative = jnp.minimum(slack, 0.0)
            coarse = negative.astype(narrow).astype(f32)
            over = jnp.where(even_at == 64, even, 0.0)
            for q, v in enumerate((over, coarse, negative - coarse)):
                tail[:, q, lanes] = v
            return jnp.minimum(low, slack)

        start = jnp.full((SUBS, LANES), jnp.inf, f32)
        low = lax.fori_loop(0, steps, body, start, unroll=4)
        low = jnp.min(jnp.min(low, axis=1, keepdims=True), axis=0, keepdims=True)
        least[r : r + 1] = jnp.broadcast_to(low, (1, LANES))

    iota = lax.broadcasted_iota(jnp.int32, (PACK, depth), 0).astype(f32).astype(narrow)
    zero = jnp.zeros((PACK, depth), narrow)
    width = 4 * GROUPS
    code_iota = lax.broadcasted_iota(jnp.int32, (LANES, width), 1).astype(f32).astype(narrow)
    code_zero = jnp.zeros((LANES, width), narrow)
    code_one = jnp.ones((LANES, width), narrow)

    def product(first, last):
        def body(s, carry):
            def spread(q):
                row = marks[q, pl.ds(s, 1), :]
                return jnp.broadcast_to(row, (PACK, depth)).astype(narrow)

            even_at, odd_at, even, odd = (spread(q) for q in range(FIELDS))
            left = []
            for at, v in ((even_at, even), (odd_at, odd)):
                for start in range(0, 64, PACK):
                    left.append(jnp.where(at == iota + narrow(start), v, zero))
            rest = jnp.concatenate([tail[s], jnp.zeros((SUBS, depth), f32)], axis=0)
            left.append(rest.astype(narrow))
            turned = codes[pl.ds(pl.multiple_of(s * steps, SUBS), steps), :].T.astype(narrow)
            right = []
            for t in range(steps):
                code = jnp.broadcast_to(turned[:, t : t + 1], (LANES, width))
                right.append(jnp.where(code == code_iota, code_one, code_zero))
            acc[...] += lax.dot_general(
                jnp.concatenate(left, axis=0),
                jnp.concatenate(right, axis=0),
                (((1,), (0,)), ((), ())),
                preferred_element_type=f32,
            )
            return carry

        lax.fori_loop(first, last, body, 0)

    lane = lax.broadcasted_iota(jnp.int32, (1, width), 1)

    def fold(v):
        v = v[:, :LANES] + v[:, LANES:]
        return v + pltpu.roll(jnp.broadcast_to(v, (SUBS, LANES)), GROUPS, 1)[0:1]

    def settle(r):
        full = acc[LANES : LANES + SUBS]
        over = pltpu.roll(jnp.broadcast_to(full[0:1], (SUBS, width)), GROUPS, 1)[0:1]
        acc[0:1] += jnp.where(lane >= GROUPS, over, 0.0)
        turned = acc[0:LANES].T
        for x in range(PAIR):
            for z in range(line):
                for g in range(4):
                    top = g * GROUPS + (x * line + z) * chunk
                    hist[r, x, z, :, g * LANES : (g + 1) * LANES] = turned[top : top + chunk]
        stats[r : r + 1] = fold(full[1:2] + full[2:3])
        if r == 0:
            stats[combos : combos + 1] = fold(full[3:4])

    def pair_of(z):
        return {"ep": z * PAIR + other}

    def line_of(z):
        return {"ep": z * PAIR + mx}

    weave_lane = lax.broadcasted_iota(jnp.int32, (chunk, LANES), 1)
    weave = (weave_lane >> 1) + (weave_lane & 1) * 64

    def finished(r, total):
        for g in range(4):
            at = slice(g * LANES, (g + 1) * LANES)
            hist_out[r, mine, :, at] = pick(total[:, at], weave) * density

    done = []

    def pair_send(r):
        return send(hist.at[r, other], pair_in.at[r], ps.at[r], pr.at[r], pair_of(mz))

    def line_send(r, copy):
        copy.wait_recv()
        hist[r, mx] += pair_in[r]
        copies = []
        for d in range(1, line):
            t = lax.rem(mz + d, line)
            copies.append(
                send(hist.at[r, mx, t], line_in.at[r, d], ls.at[r, d], lr.at[r, d], line_of(t))
            )
        done.append(copy)
        return copies

    def line_gather(r, copies):
        total = hist[r, mx, mz]
        for d in range(1, line):
            copies[d - 1].wait_recv()
            total += line_in[r, d]
        finished(r, total)
        part = hist_out.at[r, mine]
        back = [send(part, part, fs.at[r, 0], fr.at[r, 0], pair_of(mz))]
        for d in range(1, line):
            t = lax.rem(mz + d, line)
            back.append(send(part, part, gs.at[r, d], gr.at[r, d], line_of(t)))
        done.extend(copies)
        return back

    def forward(r, back):
        ends = [back[0]]
        for d in range(1, line):
            back[d].wait_recv()
            part = hist_out.at[r, mx * line + lax.rem(mz + line - d, line)]
            ends.append(send(part, part, fs.at[r, d], fr.at[r, d], pair_of(mz)))
        return back[1:], ends

    def all_send(r):
        copies = []
        for d in range(1, n):
            t = lax.rem(me + d, n)
            src = hist.at[r, lax.rem(t, PAIR), t // PAIR]
            copies.append(send(src, all_in.at[d], ls.at[r, d], lr.at[r, d], {"ep": t}))
        return copies

    def all_gather(r, copies):
        total = hist[r, mx, mz]
        for d in range(1, n):
            copies[d - 1].wait_recv()
            total += all_in[d]
        finished(r, total)
        part = hist_out.at[r, mine]
        back = []
        for d in range(1, n):
            t = lax.rem(me + d, n)
            back.append(send(part, part, gs.at[r, d], gr.at[r, d], {"ep": t}))
        done.extend(copies)
        return back

    row = lax.broadcasted_iota(jnp.int32, (SUBS, SUBS, depth), 1)
    tail[...] = jnp.where(row == 3, 1.0, 0.0).astype(f32)
    stats[...] = jnp.zeros_like(stats)

    paired, lined, backs, ended, all_sent = {}, {}, {}, {}, {}
    sent_only = []
    spread_out = []
    half = SUBS // 2

    def progress(slot):
        for action, r in plan.get(slot, ()):
            if action == "line":
                lined[r] = line_send(r, paired[r])
            elif action == "gather":
                backs[r] = line_gather(r, lined[r])
            elif action == "forward":
                got, ends = forward(r, backs[r])
                sent_only.extend(got)
                ended[r] = ends
            elif action == "worst":
                for copy in mins:
                    copy.wait_recv()
                low = worst[rows_of(mc)]
                for d in range(1, nc):
                    low = jnp.minimum(low, worst_in[d])
                worst_out[rows_of(mc)] = low
                for d in range(1, nc):
                    t = lax.rem(mc + d, nc)
                    part = worst_out.at[rows_of(mc)]
                    spread_out.append(send(part, part, vs.at[d], vr.at[d], {"corner": t}))

    for r in range(combos):
        find(r)
        acc[...] = jnp.zeros_like(acc)
        progress((r, 0))
        product(0, half)
        progress((r, 1))
        product(half, SUBS)
        settle(r)
        if r == combos - 1:
            all_sent[r] = all_send(r)
        else:
            paired[r] = pair_send(r)
        progress((r, 2))

    stats[combos * 2 : combos * 3] = least[0:combos]
    shares = []
    for d in range(1, n):
        t = lax.rem(me + d, n)
        shares.append(send(stats, stats_in.at[me], ss.at[d], sr.at[d], {"ep": t}))
    progress("end0")
    last = all_gather(combos - 1, all_sent[combos - 1])
    progress("end1")
    for copy in shares:
        copy.wait_recv()
    stats_in[me] = stats[...]
    added = stats_in[0, 0 : 2 * combos]
    lowest = stats_in[0, 2 * combos : 3 * combos]
    for k in range(1, n):
        added += stats_in[k, 0 : 2 * combos]
        lowest = jnp.minimum(lowest, stats_in[k, 2 * combos : 3 * combos])
    stats_out[0 : 2 * combos] = added
    stats_out[2 * combos : 3 * combos] = lowest
    for copy in spread_out + last:
        copy.wait_recv()
    for r in ended:
        for copy in ended[r]:
            copy.wait_recv()
    for copy in mins + done + sent_only + shares + spread_out + last:
        copy.wait_send()
    for r in ended:
        for copy in ended[r]:
            copy.wait_send()


def finish_kernel(endpoints, hist, stats, worst, hist_out, tns_out, share_out, total_out, least_out, worst_out):
    corners = total_out.shape[0]
    combos = 2 * corners
    share = GROUPS / endpoints
    for m in range(2):
        for c in range(corners):
            r = m * corners + c
            hist_out[:, c, m, :] = hist[r]
            row = stats[r : r + 1, :GROUPS]
            tns_out[c, m : m + 1, :] = row * share
            total = jnp.sum(row, axis=1, keepdims=True) * (1.0 / endpoints)
            total_out[c : c + 1, m : m + 1] = total
            least_out[c : c + 1, m : m + 1] = stats[2 * combos + r : 2 * combos + r + 1, 0:1]
    share_out[...] = stats[combos : combos + 1, :GROUPS] * share
    worst_out[...] = worst[...]


def make_plan(combos):
    plan = {(0, 1): [("worst", 0)]}
    for r in range(combos - 1):
        places = [(r + 1, 1), (r + 2, 0), (r + 2, 2)]
        for action, (q, part) in zip(("line", "gather", "forward"), places):
            key = (q, part) if q < combos else ("end0" if action == "gather" else "end1")
            plan.setdefault(key, []).append((action, r))
    return plan


def on_device(required, arrival, hold_required, early_arrival, part_ids, bin_edges):
    corners, rows = required.shape
    n, nc = lax.axis_size("ep"), lax.axis_size("corner")
    endpoints = rows * n
    bins = bin_edges.shape[0]
    combos = 2 * corners
    blocks = rows // LANES
    steps = blocks // SUBS
    depth = steps * LANES
    line = n // PAIR
    chunk = GROUPS // n
    f32 = jnp.float32

    def by_block(v):
        return v.reshape(corners, blocks, LANES).transpose(1, 0, 2).reshape(blocks * corners, LANES)

    vmem = pl.BlockSpec(memory_space=pltpu.VMEM)
    dma = pltpu.SemaphoreType.DMA
    hist, stats, worst = pl.pallas_call(
        functools.partial(report_kernel, n, nc, GROUPS * bins / endpoints, make_plan(combos)),
        out_shape=(
            jax.ShapeDtypeStruct((combos, n, chunk, bins), f32),
            jax.ShapeDtypeStruct((3 * combos, LANES), f32),
            jax.ShapeDtypeStruct((2 * blocks, LANES), f32),
        ),
        in_specs=[vmem] * 6,
        out_specs=[vmem] * 3,
        scratch_shapes=[
            pltpu.VMEM((FIELDS, SUBS, depth), f32),
            pltpu.VMEM((blocks, LANES), f32),
            pltpu.VMEM((SUBS, SUBS, depth), f32),
            pltpu.VMEM((LANES + PACK, 4 * GROUPS), f32),
            pltpu.VMEM((2 * blocks, LANES), f32),
            pltpu.VMEM((nc, 2 * blocks // nc, LANES), f32),
            pltpu.VMEM((combos, LANES), f32),
            pltpu.VMEM((combos, PAIR, line, chunk, bins), f32),
            pltpu.VMEM((combos, line, chunk, bins), f32),
            pltpu.VMEM((combos, line, chunk, bins), f32),
            pltpu.VMEM((n, chunk, bins), f32),
            pltpu.VMEM((3 * combos, LANES), f32),
            pltpu.VMEM((n, 3 * combos, LANES), f32),
        ]
        + [dma((combos,))] * 2
        + [dma((combos, n))] * 6
        + [dma((n,))] * 2
        + [dma((nc,))] * 4,
        compiler_params=pltpu.CompilerParams(collective_id=0, has_side_effects=True),
        name="report",
    )(
        by_block(required), by_block(arrival), by_block(hold_required), by_block(early_arrival),
        part_ids.reshape(blocks, LANES), bin_edges.reshape(bins // LANES, LANES),
    )
    worst = worst.reshape(blocks, 2, LANES).transpose(1, 0, 2).reshape(2, rows)
    part_hist, part_tns, part_share, tns, wns, worst = pl.pallas_call(
        functools.partial(finish_kernel, endpoints),
        out_shape=(
            jax.ShapeDtypeStruct((GROUPS, corners, 2, bins), f32),
            jax.ShapeDtypeStruct((corners, 2, GROUPS), f32),
            jax.ShapeDtypeStruct((1, GROUPS), f32),
            jax.ShapeDtypeStruct((corners, 2), f32),
            jax.ShapeDtypeStruct((corners, 2), f32),
            jax.ShapeDtypeStruct((2, rows), f32),
        ),
        in_specs=[vmem] * 3,
        out_specs=[vmem] * 6,
        name="finish",
    )(hist.reshape(combos, GROUPS, bins), stats, worst)
    return (part_hist, part_tns.transpose(2, 0, 1), part_share[0], tns, wns, worst)


def solution(mesh):
    in_specs = (
        P("corner", "ep"),
        P("corner", "ep"),
        P("corner", "ep"),
        P("corner", "ep"),
        P("ep"),
        P(),
    )
    out_specs = (
        P(None, "corner", None, None),
        P(None, "corner", None),
        P(),
        P("corner", None),
        P("corner", None),
        P(None, "ep"),
    )
    return jax.shard_map(
        on_device, mesh=mesh, in_specs=in_specs, out_specs=out_specs, check_vma=False
    )
```

time: 65.1 us -> 70 us (1.075)
  Pallas kernels: 64.2 us -> 67.3 us
  local copies, waits for them, and re-layouts: 0 us -> 1.86 us
    pallas_call x1, Pallas kernels: 52 us -> 65.2 us  [on_device(): pl.pallas_call(functools.partial(report_kernel, n, nc, GROUPS * bins / en...]
    pallas_call x1 -> x0, Pallas kernels: 10.1 us -> none  [on_device(): pl.pallas_call(search_kernel, out_shape=(jax.ShapeDtypeStruct((5, combos,...]
    reshape x0 -> x1, local copies, waits for them, and re-layouts: none -> 0.97 us  [on_device(): worst = worst.reshape(blocks, 2, LANES).transpose(1, 0, 2).reshape(2, rows)]
    unnamed x0 -> x1, local copies, waits for them, and re-layouts: none -> 0.89 us
where the time goes in v1:
time: 70 us; the launch traced here: 69.8 us
  Pallas kernels  67.3 us (96%)
  local copies, waits for them, and re-layouts  1.86 us (3%)
    pallas_call x1, Pallas kernels, on_device(): pl.pallas_call(functools.partial(report_kernel, n, nc, GROUPS * bins / en...  65.2 us
    pallas_call x1, Pallas kernels, on_device(): pl.pallas_call(functools.partial(finish_kernel, endpoints), out_shape=(ja...  2.11 us

profile of v1, /device:TPU:0, one launch (start us, length us, event | category | flops | bytes accessed | tf_op | source)
XLA Modules:
  0.0 69.8 jit_solution(11692914682448438527)
XLA Ops:
  0.6 65.2 %report.1 = (f32[4,8,8,512]{3,2,1,0:T(8,128)}, f32[12,128]{1,0:T(8,128)}, f32[512,128]{1,0:T(8,128)}) custom-call(f32[512,128]{1,0:T(8,128)} %bitcast.37, f32[512,128]{1,0:T(8,128)} %bitcast.38, f32[512,128]{1,0:T(8,128)} %bitcast.39, f32[512,128]{1,0:T(8,128)} %bitcast.40, s32[256,128]{1,0:T(8,128)} %bitcast.41, s32[4,128]{1,0:T(4,128)} %bitcast.42), custom_call_target="tpu_custom_call" | custom-call | tf_op jit(solution)/shard_map/report/pallas_call | solution.py:422
  65.8 1.0 %copy.21 = f32[256,2,128]{2,0,1:T(8,128)S(1)} copy(f32[256,2,128]{2,1,0:T(2,128)} %bitcast.36) | data formatting | bytes 524288 | tf_op jit(solution)/shard_map/reshape | solution.py:456
  66.8 0.9 %copy.20 = f32[1,2,256,128]{3,1,2,0:T(2,128)} copy(f32[1,2,256,128]{3,2,1,0:T(8,128)S(1)} %bitcast.34) | data formatting | bytes 524288
  67.7 2.1 %finish.1 = (f32[64,2,2,512]{3,2,1,0:T(2,128)}, f32[2,2,64]{2,1,0:T(2,128)}, f32[1,64]{1,0:T(1,128)}, f32[2,2]{1,0:T(2,128)}, f32[2,2]{1,0:T(2,128)}, /*index=5*/f32[2,32768]{1,0:T(2,128)}) custom-call(f32[4,64,512]{2,1,0:T(8,128)} %bitcast.35, f32[12,128]{1,0:T(8,128)} %get-tuple-element.16.stats, f32[2,32768]{1,0:T(2,128)} %bitcast.33), custom_call_target="tpu_custom_call" | custom-call | tf_op jit(solution)/shard_map/finish/pallas_call | solution.py:457

commit v2 on v1

--- a/solution.py
+++ b/solution.py
@@ -9,6 +9,7 @@
 GROUPS = 64
 LANES = 128
 SUBS = 8
+SPAN = 32
 PACK = 16
 PAIR = 2
 FIELDS = 4
@@ -76,7 +77,7 @@
 
 
 def report_kernel(
-    n, nc, density, plan,
+    n, nc, density, plan, accs,
     req, arr, hreq, early, ids, edges,
     hist_out, stats_out, worst_out,
     marks, codes, tail, acc, worst, worst_in, least,
@@ -87,7 +88,6 @@
     combos = 2 * corners
     blocks = ids.shape[0]
     steps = blocks // SUBS
-    depth = steps * LANES
     chunk = GROUPS // n
     line = n // PAIR
     share = worst_out.shape[0] // nc
@@ -147,30 +147,29 @@
         plus, minus = sources[kind]
 
         def body(step, low):
-            at = pl.ds(corners * step + c, SUBS, stride=corners * steps)
-            lanes = pl.ds(pl.multiple_of(step * LANES, LANES), LANES)
+            at = pl.ds(corners * SUBS * step + c, SUBS, stride=corners)
+            here = pl.ds(pl.multiple_of(step * SUBS, SUBS), SUBS)
             slack = plus[at, :] - minus[at, :]
             part, even_at, odd_at, even, odd = search(tables, slack)
-            group = ids[pl.ds(step, SUBS, stride=steps), :]
-            codes[pl.ds(step, SUBS, stride=steps), :] = (part * GROUPS + group).astype(f32)
-            for q, v in enumerate((even_at, odd_at)):
-                marks[q, :, lanes] = v.astype(f32)
-            marks[2, :, lanes] = even
-            marks[3, :, lanes] = odd
+            codes[here, :] = (part * GROUPS + ids[here, :]).astype(f32)
+            marks[0, here, :] = even_at.astype(f32)
+            marks[1, here, :] = odd_at.astype(f32)
+            marks[2, here, :] = even
+            marks[3, here, :] = odd
             negative = jnp.minimum(slack, 0.0)
             coarse = negative.astype(narrow).astype(f32)
             over = jnp.where(even_at == 64, even, 0.0)
             for q, v in enumerate((over, coarse, negative - coarse)):
-                tail[:, q, lanes] = v
+                tail[pl.ds(SUBS * SUBS * step + q, SUBS, stride=SUBS), :] = v
             return jnp.minimum(low, slack)
 
         start = jnp.full((SUBS, LANES), jnp.inf, f32)
-        low = lax.fori_loop(0, steps, body, start, unroll=4)
+        low = lax.fori_loop(0, steps, body, start, unroll=8)
         low = jnp.min(jnp.min(low, axis=1, keepdims=True), axis=0, keepdims=True)
         least[r : r + 1] = jnp.broadcast_to(low, (1, LANES))
 
-    iota = lax.broadcasted_iota(jnp.int32, (PACK, depth), 0).astype(f32).astype(narrow)
-    zero = jnp.zeros((PACK, depth), narrow)
+    iota = lax.broadcasted_iota(jnp.int32, (PACK, LANES), 0).astype(f32).astype(narrow)
+    zero = jnp.zeros((PACK, LANES), narrow)
     width = 4 * GROUPS
     code_iota = lax.broadcasted_iota(jnp.int32, (LANES, width), 1).astype(f32).astype(narrow)
     code_zero = jnp.zeros((LANES, width), narrow)
@@ -178,28 +177,44 @@
 
     def product(first, last):
         def body(s, carry):
-            def spread(q):
-                row = marks[q, pl.ds(s, 1), :]
-                return jnp.broadcast_to(row, (PACK, depth)).astype(narrow)
-
-            even_at, odd_at, even, odd = (spread(q) for q in range(FIELDS))
-            left = []
-            for at, v in ((even_at, even), (odd_at, odd)):
-                for start in range(0, 64, PACK):
-                    left.append(jnp.where(at == iota + narrow(start), v, zero))
-            rest = jnp.concatenate([tail[s], jnp.zeros((SUBS, depth), f32)], axis=0)
-            left.append(rest.astype(narrow))
-            turned = codes[pl.ds(pl.multiple_of(s * steps, SUBS), steps), :].T.astype(narrow)
-            right = []
-            for t in range(steps):
+            base = pl.multiple_of(s * SPAN, SPAN)
+            turned = codes[pl.ds(base, SPAN), :].T.astype(narrow)
+
+            def left(t):
+                def spread(q):
+                    row = marks[q, pl.ds(base + t, 1), :]
+                    return jnp.broadcast_to(row, (PACK, LANES)).astype(narrow)
+
+                even_at, odd_at, even, odd = (spread(q) for q in range(FIELDS))
+                parts = []
+                for at, v in ((even_at, even), (odd_at, odd)):
+                    for start in range(0, 64, PACK):
+                        parts.append(jnp.where(at == iota + narrow(start), v, zero))
+                rest = tail[pl.ds(pl.multiple_of(SUBS * (base + t), SUBS), SUBS), :]
+                rest = jnp.concatenate([rest, jnp.zeros((SUBS, LANES), f32)], axis=0)
+                return jnp.concatenate(parts + [rest.astype(narrow)], axis=0)
+
+            def right(t):
                 code = jnp.broadcast_to(turned[:, t : t + 1], (LANES, width))
-                right.append(jnp.where(code == code_iota, code_one, code_zero))
-            acc[...] += lax.dot_general(
-                jnp.concatenate(left, axis=0),
-                jnp.concatenate(right, axis=0),
-                (((1,), (0,)), ((), ())),
-                preferred_element_type=f32,
-            )
+                return jnp.where(code == code_iota, code_one, code_zero)
+
+            def push(p):
+                pltpu.matmul_push_rhs(
+                    jnp.concatenate([right(2 * p), right(2 * p + 1)], axis=0),
+                    staging_register=(p // 2) % 2, mxu_index=p % 2,
+                )
+
+            tiles = SPAN // 2
+            push(0)
+            push(1)
+            for p in range(tiles):
+                if p + 2 < tiles:
+                    push(p + 2)
+                pltpu.matmul_acc_lhs(
+                    accs[p % 2],
+                    jnp.concatenate([left(2 * p), left(2 * p + 1)], axis=1),
+                    load_staged_rhs=(p // 2) % 2,
+                )
             return carry
 
         lax.fori_loop(first, last, body, 0)
@@ -211,6 +226,7 @@
         return v + pltpu.roll(jnp.broadcast_to(v, (SUBS, LANES)), GROUPS, 1)[0:1]
 
     def settle(r):
+        acc[...] = pltpu.matmul_pop(accs[0]) + pltpu.matmul_pop(accs[1])
         full = acc[LANES : LANES + SUBS]
         over = pltpu.roll(jnp.broadcast_to(full[0:1], (SUBS, width)), GROUPS, 1)[0:1]
         acc[0:1] += jnp.where(lane >= GROUPS, over, 0.0)
@@ -299,14 +315,23 @@
         done.extend(copies)
         return back
 
-    row = lax.broadcasted_iota(jnp.int32, (SUBS, SUBS, depth), 1)
-    tail[...] = jnp.where(row == 3, 1.0, 0.0).astype(f32)
+    row = lax.broadcasted_iota(jnp.int32, (SUBS, LANES), 0)
+    fresh = jnp.where(row == 3, 1.0, 0.0).astype(f32)
+
+    def clear(step, carry):
+        tail[pl.ds(pl.multiple_of(SUBS * step, SUBS), SUBS), :] = fresh
+        return carry
+
+    lax.fori_loop(0, blocks, clear, 0, unroll=8)
+    pltpu.matmul_pop(accs[0])
+    pltpu.matmul_pop(accs[1])
     stats[...] = jnp.zeros_like(stats)
 
     paired, lined, backs, ended, all_sent = {}, {}, {}, {}, {}
     sent_only = []
     spread_out = []
-    half = SUBS // 2
+    whole = blocks // SPAN
+    half = whole // 2
 
     def progress(slot):
         for action, r in plan.get(slot, ()):
@@ -332,11 +357,10 @@
 
     for r in range(combos):
         find(r)
-        acc[...] = jnp.zeros_like(acc)
         progress((r, 0))
         product(0, half)
         progress((r, 1))
-        product(half, SUBS)
+        product(half, whole)
         settle(r)
         if r == combos - 1:
             all_sent[r] = all_send(r)
@@ -374,6 +398,14 @@
             copy.wait_send()
 
 
+def report(n, nc, density, plan, *refs):
+    def body(first, second):
+        report_kernel(n, nc, density, plan, (first, second), *refs)
+
+    shape = (LANES + PACK, 4 * GROUPS)
+    pl.run_scoped(body, pltpu.ACC(0)(shape, jnp.float32), pltpu.ACC(1)(shape, jnp.float32))
+
+
 def finish_kernel(endpoints, hist, stats, worst, hist_out, tns_out, share_out, total_out, least_out, worst_out):
     corners = total_out.shape[0]
     combos = 2 * corners
@@ -408,8 +440,6 @@
     bins = bin_edges.shape[0]
     combos = 2 * corners
     blocks = rows // LANES
-    steps = blocks // SUBS
-    depth = steps * LANES
     line = n // PAIR
     chunk = GROUPS // n
     f32 = jnp.float32
@@ -420,7 +450,7 @@
     vmem = pl.BlockSpec(memory_space=pltpu.VMEM)
     dma = pltpu.SemaphoreType.DMA
     hist, stats, worst = pl.pallas_call(
-        functools.partial(report_kernel, n, nc, GROUPS * bins / endpoints, make_plan(combos)),
+        functools.partial(report, n, nc, GROUPS * bins / endpoints, make_plan(combos)),
         out_shape=(
             jax.ShapeDtypeStruct((combos, n, chunk, bins), f32),
             jax.ShapeDtypeStruct((3 * combos, LANES), f32),
@@ -429,9 +459,9 @@
         in_specs=[vmem] * 6,
         out_specs=[vmem] * 3,
         scratch_shapes=[
-            pltpu.VMEM((FIELDS, SUBS, depth), f32),
+            pltpu.VMEM((FIELDS, blocks, LANES), f32),
             pltpu.VMEM((blocks, LANES), f32),
-            pltpu.VMEM((SUBS, SUBS, depth), f32),
+            pltpu.VMEM((SUBS * blocks, LANES), f32),
             pltpu.VMEM((LANES + PACK, 4 * GROUPS), f32),
             pltpu.VMEM((2 * blocks, LANES), f32),
             pltpu.VMEM((nc, 2 * blocks // nc, LANES), f32),

time: 70 us -> 54.9 us (0.78)
  Pallas kernels: 67.3 us -> 52.2 us
    pallas_call x1, Pallas kernels: 65.2 us -> 50.1 us  [on_device(): pl.pallas_call(functools.partial(report, n, nc, GROUPS * bins / endpoints...]
where the time goes in v2:
time: 54.9 us; the launch traced here: 54.7 us
  Pallas kernels  52.2 us (95%)
  local copies, waits for them, and re-layouts  1.86 us (3%)
  between operations  0.65 us (1%)
    pallas_call x1, Pallas kernels, on_device(): pl.pallas_call(functools.partial(report, n, nc, GROUPS * bins / endpoints...  50.1 us
    pallas_call x1, Pallas kernels, on_device(): pl.pallas_call(functools.partial(finish_kernel, endpoints), out_shape=(ja...  2.11 us

profile of v2, /device:TPU:0, one launch (start us, length us, event | category | flops | bytes accessed | tf_op | source)
XLA Modules:
  0.0 54.7 jit_solution(2682745030046187914)
XLA Ops:
  0.6 50.1 %report.1 = (f32[4,8,8,512]{3,2,1,0:T(8,128)}, f32[12,128]{1,0:T(8,128)}, f32[512,128]{1,0:T(8,128)}) custom-call(f32[512,128]{1,0:T(8,128)} %bitcast.37, f32[512,128]{1,0:T(8,128)} %bitcast.38, f32[512,128]{1,0:T(8,128)} %bitcast.39, f32[512,128]{1,0:T(8,128)} %bitcast.40, s32[256,128]{1,0:T(8,128)} %bitcast.41, s32[4,128]{1,0:T(4,128)} %bitcast.42), custom_call_target="tpu_custom_call" | custom-call | tf_op jit(solution)/shard_map/report/pallas_call | solution.py:452
  50.8 1.0 %copy.21 = f32[256,2,128]{2,0,1:T(8,128)S(1)} copy(f32[256,2,128]{2,1,0:T(2,128)} %bitcast.36) | data formatting | bytes 524288 | tf_op jit(solution)/shard_map/reshape | solution.py:486
  51.7 0.9 %copy.20 = f32[1,2,256,128]{3,1,2,0:T(2,128)} copy(f32[1,2,256,128]{3,2,1,0:T(8,128)S(1)} %bitcast.34) | data formatting | bytes 524288
  52.6 2.1 %finish.1 = (f32[64,2,2,512]{3,2,1,0:T(2,128)}, f32[2,2,64]{2,1,0:T(2,128)}, f32[1,64]{1,0:T(1,128)}, f32[2,2]{1,0:T(2,128)}, f32[2,2]{1,0:T(2,128)}, /*index=5*/f32[2,32768]{1,0:T(2,128)}) custom-call(f32[4,64,512]{2,1,0:T(8,128)} %bitcast.35, f32[12,128]{1,0:T(8,128)} %get-tuple-element.16.stats, f32[2,32768]{1,0:T(2,128)} %bitcast.33), custom_call_target="tpu_custom_call" | custom-call | tf_op jit(solution)/shard_map/finish/pallas_call | solution.py:487

commit v3 on v2

--- a/solution.py
+++ b/solution.py
@@ -10,6 +10,7 @@
 LANES = 128
 SUBS = 8
 SPAN = 32
+AHEAD = 4
 PACK = 16
 PAIR = 2
 FIELDS = 4
@@ -35,41 +36,48 @@
     def same(row):
         return pick(row, jnp.zeros((SUBS, LANES), jnp.int32))
 
+    eighths = [same(rows[k // 2]) if k % 2 == 0 else gathered(jnp.full((SUBS, LANES), 64 * k, jnp.int32)) for k in range(8)]
     steps = []
-    for k in range(2, 8):
-        steps.append(gathered(((lane << (9 - k)) + (1 << (8 - k))) & 511))
-    last = [gathered(2 * lane + 1), gathered(2 * lane + 2 * LANES + 1)]
-    return [same(row) for row in rows], steps, last
+    for size in (16, 4, 1):
+        steps.append([gathered((4 * size * lane + size * j) & 511) for j in (1, 2, 3)])
+    return eighths, steps
 
 
 def search(tables, slack):
-    quarter, steps, last = tables
-    level = jnp.minimum(jnp.maximum(slack, quarter[0]), 0.0)
-    top = level >= quarter[2]
-    low = jnp.where(top, quarter[2], quarter[0])
-    high = jnp.where(top, 0.0, quarter[2])
-    value = jnp.where(top, quarter[3], quarter[1])
+    eighths, steps = tables
+    level = jnp.minimum(jnp.maximum(slack, eighths[0]), 0.0)
+    top = level >= eighths[4]
+    low = jnp.where(top, eighths[4], eighths[0])
+    high = jnp.where(top, 0.0, eighths[4])
+    value = jnp.where(top, eighths[6], eighths[2])
     above = level >= value
     low = jnp.where(above, value, low)
     high = jnp.where(above, high, value)
-    index = jnp.where(top, 2, 0) + jnp.where(above, 1, 0)
-    part = index
-    for table in steps:
-        value = pick(table, index)
+    part = jnp.where(top, 2, 0) + jnp.where(above, 1, 0)
+    value = jnp.where(
+        top, jnp.where(above, eighths[7], eighths[5]), jnp.where(above, eighths[3], eighths[1])
+    )
+    above = level >= value
+    low = jnp.where(above, value, low)
+    high = jnp.where(above, high, value)
+    index = part + part
+    index = jnp.where(above, index + 1, index)
+    for first_at, middle, last_at in steps:
+        value = pick(middle, index)
+        top = level >= value
+        low = jnp.where(top, value, low)
+        high = jnp.where(top, high, value)
+        value = jnp.where(top, pick(last_at, index), pick(first_at, index))
         above = level >= value
         low = jnp.where(above, value, low)
         high = jnp.where(above, high, value)
-        index = index + index
+        index = 4 * index
+        index = jnp.where(top, index + 2, index)
         index = jnp.where(above, index + 1, index)
-    place = index & (LANES - 1)
-    value = jnp.where(top, pick(last[1], place), pick(last[0], place))
-    above = level >= value
-    low = jnp.where(above, value, low)
-    high = jnp.where(above, high, value)
     scale = 1.0 / (high - low)
     first = (high - level) * scale
     second = (level - low) * scale
-    odd_at = index & 63
+    odd_at = (index >> 1) & 63
     even_at = jnp.where(above, odd_at + 1, odd_at)
     even = jnp.where(above, second, first)
     odd = jnp.where(above, first, second)
@@ -77,10 +85,10 @@
 
 
 def report_kernel(
-    n, nc, density, plan, accs,
+    n, nc, density, plan, accs, spare,
     req, arr, hreq, early, ids, edges,
     hist_out, stats_out, worst_out,
-    marks, codes, tail, acc, worst, worst_in, least,
+    marks, codes, turned, tail, acc, worst, worst_in, least,
     hist, pair_in, line_in, all_in, stats, stats_in,
     ps, pr, ls, lr, gs, gr, fs, fr, ss, sr, ws, wr, vs, vr,
 ):
@@ -167,6 +175,8 @@
         low = lax.fori_loop(0, steps, body, start, unroll=8)
         low = jnp.min(jnp.min(low, axis=1, keepdims=True), axis=0, keepdims=True)
         least[r : r + 1] = jnp.broadcast_to(low, (1, LANES))
+        for s in range(blocks // SPAN):
+            turned[s, :, :SPAN] = codes[s * SPAN : (s + 1) * SPAN].T
 
     iota = lax.broadcasted_iota(jnp.int32, (PACK, LANES), 0).astype(f32).astype(narrow)
     zero = jnp.zeros((PACK, LANES), narrow)
@@ -175,49 +185,60 @@
     code_zero = jnp.zeros((LANES, width), narrow)
     code_one = jnp.ones((LANES, width), narrow)
 
+    tiles = SPAN // 2
+    whole = blocks // SPAN
+
+    def push(columns, p):
+        parts = []
+        for t in (2 * p, 2 * p + 1):
+            code = jnp.broadcast_to(columns[:, t : t + 1], (LANES, width))
+            parts.append(jnp.where(code == code_iota, code_one, code_zero))
+        pltpu.matmul_push_rhs(
+            jnp.concatenate(parts, axis=0), staging_register=(p // 2) % 2, mxu_index=p % 2
+        )
+
+    def left(at):
+        def spread(q):
+            row = marks[q, pl.ds(at, 1), :]
+            return jnp.broadcast_to(row, (PACK, LANES)).astype(narrow)
+
+        even_at, odd_at, even, odd = (spread(q) for q in range(FIELDS))
+        parts = []
+        for place, v in ((even_at, even), (odd_at, odd)):
+            for start in range(0, 64, PACK):
+                parts.append(jnp.where(place == iota + narrow(start), v, zero))
+        rest = tail[pl.ds(pl.multiple_of(SUBS * at, SUBS), SUBS), :]
+        rest = jnp.concatenate([rest, jnp.zeros((SUBS, LANES), f32)], axis=0)
+        return jnp.concatenate(parts + [rest.astype(narrow)], axis=0)
+
+    def begin():
+        columns = turned[0, :, :SPAN].astype(narrow)
+        for p in range(AHEAD):
+            push(columns, p)
+
     def product(first, last):
         def body(s, carry):
             base = pl.multiple_of(s * SPAN, SPAN)
-            turned = codes[pl.ds(base, SPAN), :].T.astype(narrow)
-
-            def left(t):
-                def spread(q):
-                    row = marks[q, pl.ds(base + t, 1), :]
-                    return jnp.broadcast_to(row, (PACK, LANES)).astype(narrow)
-
-                even_at, odd_at, even, odd = (spread(q) for q in range(FIELDS))
-                parts = []
-                for at, v in ((even_at, even), (odd_at, odd)):
-                    for start in range(0, 64, PACK):
-                        parts.append(jnp.where(at == iota + narrow(start), v, zero))
-                rest = tail[pl.ds(pl.multiple_of(SUBS * (base + t), SUBS), SUBS), :]
-                rest = jnp.concatenate([rest, jnp.zeros((SUBS, LANES), f32)], axis=0)
-                return jnp.concatenate(parts + [rest.astype(narrow)], axis=0)
-
-            def right(t):
-                code = jnp.broadcast_to(turned[:, t : t + 1], (LANES, width))
-                return jnp.where(code == code_iota, code_one, code_zero)
-
-            def push(p):
-                pltpu.matmul_push_rhs(
-                    jnp.concatenate([right(2 * p), right(2 * p + 1)], axis=0),
-                    staging_register=(p // 2) % 2, mxu_index=p % 2,
-                )
-
-            tiles = SPAN // 2
-            push(0)
-            push(1)
+            columns = turned[s, :, :SPAN].astype(narrow)
+            later = turned[jnp.minimum(s + 1, whole - 1), :, :SPAN].astype(narrow)
             for p in range(tiles):
-                if p + 2 < tiles:
-                    push(p + 2)
                 pltpu.matmul_acc_lhs(
                     accs[p % 2],
-                    jnp.concatenate([left(2 * p), left(2 * p + 1)], axis=1),
+                    jnp.concatenate([left(base + 2 * p), left(base + 2 * p + 1)], axis=1),
                     load_staged_rhs=(p // 2) % 2,
                 )
+                if p + AHEAD < tiles:
+                    push(columns, p + AHEAD)
+                else:
+                    push(later, p + AHEAD - tiles)
             return carry
 
         lax.fori_loop(first, last, body, 0)
+
+    def drain():
+        nothing = jnp.zeros((PACK, width), narrow)
+        for p in range(AHEAD):
+            pltpu.matmul_acc_lhs(spare[p % 2], nothing, load_staged_rhs=(p // 2) % 2)
 
     lane = lax.broadcasted_iota(jnp.int32, (1, width), 1)
 
@@ -226,6 +247,7 @@
         return v + pltpu.roll(jnp.broadcast_to(v, (SUBS, LANES)), GROUPS, 1)[0:1]
 
     def settle(r):
+        drain()
         acc[...] = pltpu.matmul_pop(accs[0]) + pltpu.matmul_pop(accs[1])
         full = acc[LANES : LANES + SUBS]
         over = pltpu.roll(jnp.broadcast_to(full[0:1], (SUBS, width)), GROUPS, 1)[0:1]
@@ -325,12 +347,13 @@
     lax.fori_loop(0, blocks, clear, 0, unroll=8)
     pltpu.matmul_pop(accs[0])
     pltpu.matmul_pop(accs[1])
+    pltpu.matmul_pop(spare[0])
+    pltpu.matmul_pop(spare[1])
     stats[...] = jnp.zeros_like(stats)
 
     paired, lined, backs, ended, all_sent = {}, {}, {}, {}, {}
     sent_only = []
     spread_out = []
-    whole = blocks // SPAN
     half = whole // 2
 
     def progress(slot):
@@ -357,6 +380,7 @@
 
     for r in range(combos):
         find(r)
+        begin()
         progress((r, 0))
         product(0, half)
         progress((r, 1))
@@ -399,11 +423,15 @@
 
 
 def report(n, nc, density, plan, *refs):
-    def body(first, second):
-        report_kernel(n, nc, density, plan, (first, second), *refs)
-
-    shape = (LANES + PACK, 4 * GROUPS)
-    pl.run_scoped(body, pltpu.ACC(0)(shape, jnp.float32), pltpu.ACC(1)(shape, jnp.float32))
+    def body(*units):
+        report_kernel(n, nc, density, plan, units[:2], units[2:], *refs)
+
+    units = [
+        pltpu.ACC(q)((rows, 4 * GROUPS), jnp.float32)
+        for rows in (LANES + PACK, PACK)
+        for q in range(2)
+    ]
+    pl.run_scoped(body, *units)
 
 
 def finish_kernel(endpoints, hist, stats, worst, hist_out, tns_out, share_out, total_out, least_out, worst_out):
@@ -461,6 +489,7 @@
         scratch_shapes=[
             pltpu.VMEM((FIELDS, blocks, LANES), f32),
             pltpu.VMEM((blocks, LANES), f32),
+            pltpu.VMEM((blocks // SPAN, LANES, LANES), f32),
             pltpu.VMEM((SUBS * blocks, LANES), f32),
             pltpu.VMEM((LANES + PACK, 4 * GROUPS), f32),
             pltpu.VMEM((2 * blocks, LANES), f32),

time: 54.9 us -> 49.9 us (0.909)
  Pallas kernels: 52.2 us -> 47.2 us
    pallas_call x1, Pallas kernels: 50.1 us -> 45.1 us  [on_device(): pl.pallas_call(functools.partial(report, n, nc, GROUPS * bins / endpoints...]
where the time goes in v3:
time: 49.9 us; the launch traced here: 49.7 us
  Pallas kernels  47.2 us (95%)
  local copies, waits for them, and re-layouts  1.86 us (4%)
  between operations  0.65 us (1%)
    pallas_call x1, Pallas kernels, on_device(): pl.pallas_call(functools.partial(report, n, nc, GROUPS * bins / endpoints...  45.1 us
    pallas_call x1, Pallas kernels, on_device(): pl.pallas_call(functools.partial(finish_kernel, endpoints), out_shape=(ja...  2.11 us

profile of v3, /device:TPU:0, one launch (start us, length us, event | category | flops | bytes accessed | tf_op | source)
XLA Modules:
  0.0 49.7 jit_solution(7522968325187236130)
XLA Ops:
  0.6 45.1 %report.1 = (f32[4,8,8,512]{3,2,1,0:T(8,128)}, f32[12,128]{1,0:T(8,128)}, f32[512,128]{1,0:T(8,128)}) custom-call(f32[512,128]{1,0:T(8,128)} %bitcast.37, f32[512,128]{1,0:T(8,128)} %bitcast.38, f32[512,128]{1,0:T(8,128)} %bitcast.39, f32[512,128]{1,0:T(8,128)} %bitcast.40, s32[256,128]{1,0:T(8,128)} %bitcast.41, s32[4,128]{1,0:T(4,128)} %bitcast.42), custom_call_target="tpu_custom_call" | custom-call | tf_op jit(solution)/shard_map/report/pallas_call | solution.py:480
  45.8 1.0 %copy.21 = f32[256,2,128]{2,0,1:T(8,128)S(1)} copy(f32[256,2,128]{2,1,0:T(2,128)} %bitcast.36) | data formatting | bytes 524288 | tf_op jit(solution)/shard_map/reshape | solution.py:515
  46.7 0.9 %copy.20 = f32[1,2,256,128]{3,1,2,0:T(2,128)} copy(f32[1,2,256,128]{3,2,1,0:T(8,128)S(1)} %bitcast.34) | data formatting | bytes 524288
  47.6 2.1 %finish.1 = (f32[64,2,2,512]{3,2,1,0:T(2,128)}, f32[2,2,64]{2,1,0:T(2,128)}, f32[1,64]{1,0:T(1,128)}, f32[2,2]{1,0:T(2,128)}, f32[2,2]{1,0:T(2,128)}, /*index=5*/f32[2,32768]{1,0:T(2,128)}) custom-call(f32[4,64,512]{2,1,0:T(8,128)} %bitcast.35, f32[12,128]{1,0:T(8,128)} %get-tuple-element.16.stats, f32[2,32768]{1,0:T(2,128)} %bitcast.33), custom_call_target="tpu_custom_call" | custom-call | tf_op jit(solution)/shard_map/finish/pallas_call | solution.py:516

commit v4 on v3

--- a/solution.py
+++ b/solution.py
@@ -86,8 +86,9 @@
 
 def report_kernel(
     n, nc, density, plan, accs, spare,
-    req, arr, hreq, early, ids, edges,
+    req_hbm, arr_hbm, hreq_hbm, early_hbm, ids_hbm, edges_hbm,
     hist_out, stats_out, worst_out,
+    req, arr, hreq, early, ids, edges, into,
     marks, codes, turned, tail, acc, worst, worst_in, least,
     hist, pair_in, line_in, all_in, stats, stats_in,
     ps, pr, ls, lr, gs, gr, fs, fr, ss, sr, ws, wr, vs, vr,
@@ -108,6 +109,13 @@
     other = PAIR - 1 - mx
     mine = mx * line + mz
 
+    loads = []
+    for k, (src, dst) in enumerate((
+        (edges_hbm, edges), (req_hbm, req), (arr_hbm, arr), (ids_hbm, ids), (early_hbm, early), (hreq_hbm, hreq)
+    )):
+        loads.append(pltpu.make_async_copy(src, dst, into.at[k]))
+        loads[-1].start()
+
     barrier = pltpu.get_barrier_semaphore()
     for d in range(1, n):
         pl.semaphore_signal(
@@ -126,29 +134,39 @@
         copy.start()
         return copy
 
+    def rows_of(k):
+        return pl.ds(pl.multiple_of(k * share, SUBS), share)
+
+    row = lax.broadcasted_iota(jnp.int32, (SUBS, LANES), 0)
+    fresh = jnp.where(row == 3, 1.0, 0.0).astype(f32)
+
+    def clear(step, carry):
+        tail[pl.ds(pl.multiple_of(SUBS * step, SUBS), SUBS), :] = fresh
+        return carry
+
+    lax.fori_loop(0, blocks, clear, 0, unroll=8)
+    loads[0].wait()
     tables = make_tables(edges)
     sources = ((req, arr), (early, hreq))
 
-    def smallest(step, carry):
-        for kind, (plus, minus) in enumerate(sources):
-            low = None
-            for c in range(corners):
-                at = pl.ds(corners * SUBS * step + c, SUBS, stride=corners)
-                slack = plus[at, :] - minus[at, :]
-                low = slack if low is None else jnp.minimum(low, slack)
-            worst[pl.ds(2 * SUBS * step + kind, SUBS, stride=2), :] = low
-        return carry
-
-    lax.fori_loop(0, steps, smallest, 0, unroll=4)
-    pl.semaphore_wait(barrier, n - 1 + nc - 1)
-
-    def rows_of(k):
-        return pl.ds(pl.multiple_of(k * share, SUBS), share)
-
     mins = []
-    for d in range(1, nc):
-        t = lax.rem(mc + d, nc)
-        mins.append(send(worst.at[rows_of(t)], worst_in.at[d], ws.at[d], wr.at[d], {"corner": t}))
+
+    def share_worst():
+        def smallest(step, carry):
+            for kind, (plus, minus) in enumerate(sources):
+                low = None
+                for c in range(corners):
+                    at = pl.ds(corners * SUBS * step + c, SUBS, stride=corners)
+                    slack = plus[at, :] - minus[at, :]
+                    low = slack if low is None else jnp.minimum(low, slack)
+                worst[pl.ds(2 * SUBS * step + kind, SUBS, stride=2), :] = low
+            return carry
+
+        lax.fori_loop(0, steps, smallest, 0, unroll=4)
+        pl.semaphore_wait(barrier, n - 1 + nc - 1)
+        for d in range(1, nc):
+            t = lax.rem(mc + d, nc)
+            mins.append(send(worst.at[rows_of(t)], worst_in.at[d], ws.at[d], wr.at[d], {"corner": t}))
 
     def find(r):
         kind, c = r // corners, r % corners
@@ -337,14 +355,6 @@
         done.extend(copies)
         return back
 
-    row = lax.broadcasted_iota(jnp.int32, (SUBS, LANES), 0)
-    fresh = jnp.where(row == 3, 1.0, 0.0).astype(f32)
-
-    def clear(step, carry):
-        tail[pl.ds(pl.multiple_of(SUBS * step, SUBS), SUBS), :] = fresh
-        return carry
-
-    lax.fori_loop(0, blocks, clear, 0, unroll=8)
     pltpu.matmul_pop(accs[0])
     pltpu.matmul_pop(accs[1])
     pltpu.matmul_pop(spare[0])
@@ -379,7 +389,14 @@
                     spread_out.append(send(part, part, vs.at[d], vr.at[d], {"corner": t}))
 
     for r in range(combos):
+        if r == 0:
+            for load in loads[1:4]:
+                load.wait()
         find(r)
+        if r == 0:
+            for load in loads[4:]:
+                load.wait()
+            share_worst()
         begin()
         progress((r, 0))
         product(0, half)
@@ -448,11 +465,12 @@
             total_out[c : c + 1, m : m + 1] = total
             least_out[c : c + 1, m : m + 1] = stats[2 * combos + r : 2 * combos + r + 1, 0:1]
     share_out[...] = stats[combos : combos + 1, :GROUPS] * share
-    worst_out[...] = worst[...]
+    for j in range(worst.shape[0] // 2):
+        worst_out[:, j * LANES : (j + 1) * LANES] = worst[2 * j : 2 * j + 2, :]
 
 
 def make_plan(combos):
-    plan = {(0, 1): [("worst", 0)]}
+    plan = {(1, 0): [("worst", 0)]}
     for r in range(combos - 1):
         places = [(r + 1, 1), (r + 2, 0), (r + 2, 2)]
         for action, (q, part) in zip(("line", "gather", "forward"), places):
@@ -484,9 +502,13 @@
             jax.ShapeDtypeStruct((3 * combos, LANES), f32),
             jax.ShapeDtypeStruct((2 * blocks, LANES), f32),
         ),
-        in_specs=[vmem] * 6,
+        in_specs=[pl.BlockSpec(memory_space=pltpu.HBM)] * 6,
         out_specs=[vmem] * 3,
-        scratch_shapes=[
+        scratch_shapes=[pltpu.VMEM((corners * blocks, LANES), f32)] * 4
+        + [
+            pltpu.VMEM((blocks, LANES), jnp.int32),
+            pltpu.VMEM((bins // LANES, LANES), jnp.int32),
+            dma((6,)),
             pltpu.VMEM((FIELDS, blocks, LANES), f32),
             pltpu.VMEM((blocks, LANES), f32),
             pltpu.VMEM((blocks // SPAN, LANES, LANES), f32),
@@ -506,13 +528,20 @@
         + [dma((combos, n))] * 6
         + [dma((n,))] * 2
         + [dma((nc,))] * 4,
-        compiler_params=pltpu.CompilerParams(collective_id=0, has_side_effects=True),
+        compiler_params=pltpu.CompilerParams(
+            collective_id=0, has_side_effects=True, vmem_limit_bytes=24 * 1024 * 1024
+        ),
         name="report",
     )(
-        by_block(required), by_block(arrival), by_block(hold_required), by_block(early_arrival),
-        part_ids.reshape(blocks, LANES), bin_edges.reshape(bins // LANES, LANES),
+        *[
+            pltpu.with_memory_space_constraint(v, pltpu.HBM)
+            for v in (
+                by_block(required), by_block(arrival), by_block(hold_required),
+                by_block(early_arrival), part_ids.reshape(blocks, LANES),
+                bin_edges.reshape(bins // LANES, LANES),
+            )
+        ]
     )
-    worst = worst.reshape(blocks, 2, LANES).transpose(1, 0, 2).reshape(2, rows)
     part_hist, part_tns, part_share, tns, wns, worst = pl.pallas_call(
         functools.partial(finish_kernel, endpoints),
         out_shape=(
@@ -525,6 +554,7 @@
         ),
         in_specs=[vmem] * 3,
         out_specs=[vmem] * 6,
+        compiler_params=pltpu.CompilerParams(vmem_limit_bytes=8 * 1024 * 1024),
         name="finish",
     )(hist.reshape(combos, GROUPS, bins), stats, worst)
     return (part_hist, part_tns.transpose(2, 0, 1), part_share[0], tns, wns, worst)

time: 49.9 us -> 42.1 us (0.84)
  Pallas kernels: 47.2 us -> 41.3 us
  local copies, waits for them, and re-layouts: 1.86 us -> 0 us
    pallas_call x1, Pallas kernels: 45.1 us -> 40.3 us  [on_device(): pl.pallas_call(functools.partial(report, n, nc, GROUPS * bins / endpoints...]
    pallas_call x1, Pallas kernels: 2.11 us -> 0.99 us  [on_device(): pl.pallas_call(functools.partial(finish_kernel, endpoints), out_shape=(ja...]
    reshape x1 -> x0, local copies, waits for them, and re-layouts: 0.97 us -> none  [on_device(): worst = worst.reshape(blocks, 2, LANES).transpose(1, 0, 2).reshape(2, rows)]
    unnamed x1 -> x0, local copies, waits for them, and re-layouts: 0.89 us -> none
where the time goes in v4:
time: 42.1 us; the launch traced here: 41.9 us
  Pallas kernels  41.3 us (98%)
  between operations  0.64 us (2%)
    pallas_call x1, Pallas kernels, on_device(): pl.pallas_call(functools.partial(report, n, nc, GROUPS * bins / endpoints...  40.3 us
    pallas_call x1, Pallas kernels, on_device(): pl.pallas_call(functools.partial(finish_kernel, endpoints), out_shape=(ja...  0.99 us

profile of v4, /device:TPU:0, one launch (start us, length us, event | category | flops | bytes accessed | tf_op | source)
XLA Modules:
  0.0 41.9 jit_solution(14868530731834008925)
XLA Ops:
  0.6 40.3 %report.1 = (f32[4,8,8,512]{3,2,1,0:T(8,128)S(1)}, f32[12,128]{1,0:T(8,128)S(1)}, f32[512,128]{1,0:T(8,128)S(1)}) custom-call(f32[512,128]{1,0:T(8,128)} %bitcast.26, f32[512,128]{1,0:T(8,128)} %bitcast.27, f32[512,128]{1,0:T(8,128)} %bitcast.28, f32[512,128]{1,0:T(8,128)} %bitcast.29, s32[256,128]{1,0:T(8,128)} %bitcast.30, s32[4,128]{1,0:T(4,128)} %bitcast.31), custom_call_target="tpu_custom_call" | custom-call | tf_op jit(solution)/shard_map/report/pallas_call | solution.py:498
  40.9 1.0 %finish.1 = (f32[64,2,2,512]{3,2,1,0:T(2,128)}, f32[2,2,64]{2,1,0:T(2,128)}, f32[1,64]{1,0:T(1,128)}, f32[2,2]{1,0:T(2,128)}, f32[2,2]{1,0:T(2,128)}, /*index=5*/f32[2,32768]{1,0:T(2,128)}) custom-call(f32[4,64,512]{2,1,0:T(8,128)S(1)} %bitcast.25, f32[12,128]{1,0:T(8,128)S(1)} %get-tuple-element.16.stats, f32[512,128]{1,0:T(8,128)S(1)} %get-tuple-element.17.worst), custom_call_target="tpu_custom_call" | custom-call | tf_op jit(solution)/shard_map/finish/pallas_call | solution.py:545

commit v5 on v4

--- a/solution.py
+++ b/solution.py
@@ -9,7 +9,7 @@
 GROUPS = 64
 LANES = 128
 SUBS = 8
-SPAN = 32
+SPAN = 128
 AHEAD = 4
 PACK = 16
 PAIR = 2
@@ -90,8 +90,8 @@
     hist_out, stats_out, worst_out,
     req, arr, hreq, early, ids, edges, into,
     marks, codes, turned, tail, acc, worst, worst_in, least,
-    hist, pair_in, line_in, all_in, stats, stats_in,
-    ps, pr, ls, lr, gs, gr, fs, fr, ss, sr, ws, wr, vs, vr,
+    hist, all_in, stats, stats_in,
+    ls, lr, gs, gr, fs, fr, ss, sr, ws, wr, vs, vr,
 ):
     corners = hist.shape[0] // 2
     combos = 2 * corners
@@ -190,7 +190,7 @@
             return jnp.minimum(low, slack)
 
         start = jnp.full((SUBS, LANES), jnp.inf, f32)
-        low = lax.fori_loop(0, steps, body, start, unroll=8)
+        low = lax.fori_loop(0, steps, body, start, unroll=16)
         low = jnp.min(jnp.min(low, axis=1, keepdims=True), axis=0, keepdims=True)
         least[r : r + 1] = jnp.broadcast_to(low, (1, LANES))
         for s in range(blocks // SPAN):
@@ -289,40 +289,42 @@
     weave_lane = lax.broadcasted_iota(jnp.int32, (chunk, LANES), 1)
     weave = (weave_lane >> 1) + (weave_lane & 1) * 64
 
-    def finished(r, total):
-        for g in range(4):
+    done = []
+
+    def all_send(r):
+        copies = []
+        for d in range(1, n):
+            t = lax.rem(me + d, n)
+            src = hist.at[r, lax.rem(t, PAIR), t // PAIR]
+            copies.append(send(src, all_in.at[r, d], ls.at[r, d], lr.at[r, d], {"ep": t}))
+        return copies
+
+    def all_sum(r, copies):
+        total = hist[r, mx, mz]
+        for d in range(1, n):
+            copies[d - 1].wait_recv()
+            total += all_in[r, d]
+        for g in range(total.shape[1] // LANES):
             at = slice(g * LANES, (g + 1) * LANES)
             hist_out[r, mine, :, at] = pick(total[:, at], weave) * density
-
-    done = []
-
-    def pair_send(r):
-        return send(hist.at[r, other], pair_in.at[r], ps.at[r], pr.at[r], pair_of(mz))
-
-    def line_send(r, copy):
-        copy.wait_recv()
-        hist[r, mx] += pair_in[r]
-        copies = []
-        for d in range(1, line):
-            t = lax.rem(mz + d, line)
-            copies.append(
-                send(hist.at[r, mx, t], line_in.at[r, d], ls.at[r, d], lr.at[r, d], line_of(t))
-            )
-        done.append(copy)
-        return copies
+        done.extend(copies)
+
+    def all_gather(r, copies):
+        all_sum(r, copies)
+        part = hist_out.at[r, mine]
+        back = []
+        for d in range(1, n):
+            t = lax.rem(me + d, n)
+            back.append(send(part, part, gs.at[r, d], gr.at[r, d], {"ep": t}))
+        return back
 
     def line_gather(r, copies):
-        total = hist[r, mx, mz]
-        for d in range(1, line):
-            copies[d - 1].wait_recv()
-            total += line_in[r, d]
-        finished(r, total)
+        all_sum(r, copies)
         part = hist_out.at[r, mine]
         back = [send(part, part, fs.at[r, 0], fr.at[r, 0], pair_of(mz))]
         for d in range(1, line):
             t = lax.rem(mz + d, line)
             back.append(send(part, part, gs.at[r, d], gr.at[r, d], line_of(t)))
-        done.extend(copies)
         return back
 
     def forward(r, back):
@@ -333,45 +335,25 @@
             ends.append(send(part, part, fs.at[r, d], fr.at[r, d], pair_of(mz)))
         return back[1:], ends
 
-    def all_send(r):
-        copies = []
-        for d in range(1, n):
-            t = lax.rem(me + d, n)
-            src = hist.at[r, lax.rem(t, PAIR), t // PAIR]
-            copies.append(send(src, all_in.at[d], ls.at[r, d], lr.at[r, d], {"ep": t}))
-        return copies
-
-    def all_gather(r, copies):
-        total = hist[r, mx, mz]
-        for d in range(1, n):
-            copies[d - 1].wait_recv()
-            total += all_in[d]
-        finished(r, total)
-        part = hist_out.at[r, mine]
-        back = []
-        for d in range(1, n):
-            t = lax.rem(me + d, n)
-            back.append(send(part, part, gs.at[r, d], gr.at[r, d], {"ep": t}))
-        done.extend(copies)
-        return back
-
     pltpu.matmul_pop(accs[0])
     pltpu.matmul_pop(accs[1])
     pltpu.matmul_pop(spare[0])
     pltpu.matmul_pop(spare[1])
     stats[...] = jnp.zeros_like(stats)
 
-    paired, lined, backs, ended, all_sent = {}, {}, {}, {}, {}
+    backs, ended, all_sent = {}, {}, {}
     sent_only = []
     spread_out = []
     half = whole // 2
 
     def progress(slot):
         for action, r in plan.get(slot, ()):
-            if action == "line":
-                lined[r] = line_send(r, paired[r])
-            elif action == "gather":
-                backs[r] = line_gather(r, lined[r])
+            if action == "all":
+                all_sent[r] = all_send(r)
+            elif action == "all_gather":
+                ended[r] = all_gather(r, all_sent[r])
+            elif action == "line_gather":
+                backs[r] = line_gather(r, all_sent[r])
             elif action == "forward":
                 got, ends = forward(r, backs[r])
                 sent_only.extend(got)
@@ -403,10 +385,6 @@
         progress((r, 1))
         product(half, whole)
         settle(r)
-        if r == combos - 1:
-            all_sent[r] = all_send(r)
-        else:
-            paired[r] = pair_send(r)
         progress((r, 2))
 
     stats[combos * 2 : combos * 3] = least[0:combos]
@@ -414,9 +392,7 @@
     for d in range(1, n):
         t = lax.rem(me + d, n)
         shares.append(send(stats, stats_in.at[me], ss.at[d], sr.at[d], {"ep": t}))
-    progress("end0")
-    last = all_gather(combos - 1, all_sent[combos - 1])
-    progress("end1")
+    progress("end")
     for copy in shares:
         copy.wait_recv()
     stats_in[me] = stats[...]
@@ -427,12 +403,12 @@
         lowest = jnp.minimum(lowest, stats_in[k, 2 * combos : 3 * combos])
     stats_out[0 : 2 * combos] = added
     stats_out[2 * combos : 3 * combos] = lowest
-    for copy in spread_out + last:
+    for copy in spread_out:
         copy.wait_recv()
     for r in ended:
         for copy in ended[r]:
             copy.wait_recv()
-    for copy in mins + done + sent_only + shares + spread_out + last:
+    for copy in mins + done + sent_only + shares + spread_out:
         copy.wait_send()
     for r in ended:
         for copy in ended[r]:
@@ -470,12 +446,20 @@
 
 
 def make_plan(combos):
-    plan = {(1, 0): [("worst", 0)]}
-    for r in range(combos - 1):
-        places = [(r + 1, 1), (r + 2, 0), (r + 2, 2)]
-        for action, (q, part) in zip(("line", "gather", "forward"), places):
-            key = (q, part) if q < combos else ("end0" if action == "gather" else "end1")
-            plan.setdefault(key, []).append((action, r))
+    last = combos - 1
+    plan = {(1, 0): [("worst", 0)], "end": []}
+    for r in range(combos):
+        plan[r, 2] = [("all", r)]
+        gather = [("line_gather", r)] if r < last else [("all_gather", r)]
+        if r < last - 1:
+            plan[r + 2, 0] = gather
+            if r > 0:
+                plan[r + 2, 0].append(("forward", r - 1))
+        else:
+            if r == last and last > 1:
+                plan["end"].append(("forward", last - 2))
+            plan["end"] += gather
+    plan["end"].append(("forward", last - 1))
     return plan
 
 
@@ -518,13 +502,10 @@
             pltpu.VMEM((nc, 2 * blocks // nc, LANES), f32),
             pltpu.VMEM((combos, LANES), f32),
             pltpu.VMEM((combos, PAIR, line, chunk, bins), f32),
-            pltpu.VMEM((combos, line, chunk, bins), f32),
-            pltpu.VMEM((combos, line, chunk, bins), f32),
-            pltpu.VMEM((n, chunk, bins), f32),
+            pltpu.VMEM((combos, n, chunk, bins), f32),
             pltpu.VMEM((3 * combos, LANES), f32),
             pltpu.VMEM((n, 3 * combos, LANES), f32),
         ]
-        + [dma((combos,))] * 2
         + [dma((combos, n))] * 6
         + [dma((n,))] * 2
         + [dma((nc,))] * 4,

time: 42.1 us -> 37.3 us (0.89)
  Pallas kernels: 41.3 us -> 36.4 us
    pallas_call x1, Pallas kernels: 40.3 us -> 35.5 us  [on_device(): pl.pallas_call(functools.partial(report, n, nc, GROUPS * bins / endpoints...]
where the time goes in v5:
time: 37.3 us; the launch traced here: 37.1 us
  Pallas kernels  36.4 us (98%)
  between operations  0.64 us (2%)
    pallas_call x1, Pallas kernels, on_device(): pl.pallas_call(functools.partial(report, n, nc, GROUPS * bins / endpoints...  35.5 us
    pallas_call x1, Pallas kernels, on_device(): pl.pallas_call(functools.partial(finish_kernel, endpoints), out_shape=(ja...  0.99 us

profile of v5, /device:TPU:0, one launch (start us, length us, event | category | flops | bytes accessed | tf_op | source)
XLA Modules:
  0.0 37.1 jit_solution(9892411627012690568)
XLA Ops:
  0.6 35.5 %report.1 = (f32[4,8,8,512]{3,2,1,0:T(8,128)S(1)}, f32[12,128]{1,0:T(8,128)S(1)}, f32[512,128]{1,0:T(8,128)S(1)}) custom-call(f32[512,128]{1,0:T(8,128)} %bitcast.26, f32[512,128]{1,0:T(8,128)} %bitcast.27, f32[512,128]{1,0:T(8,128)} %bitcast.28, f32[512,128]{1,0:T(8,128)} %bitcast.29, s32[256,128]{1,0:T(8,128)} %bitcast.30, s32[4,128]{1,0:T(4,128)} %bitcast.31), custom_call_target="tpu_custom_call" | custom-call | tf_op jit(solution)/shard_map/report/pallas_call | solution.py:482
  36.1 1.0 %finish.1 = (f32[64,2,2,512]{3,2,1,0:T(2,128)}, f32[2,2,64]{2,1,0:T(2,128)}, f32[1,64]{1,0:T(1,128)}, f32[2,2]{1,0:T(2,128)}, f32[2,2]{1,0:T(2,128)}, /*index=5*/f32[2,32768]{1,0:T(2,128)}) custom-call(f32[4,64,512]{2,1,0:T(8,128)S(1)} %bitcast.25, f32[12,128]{1,0:T(8,128)S(1)} %get-tuple-element.16.stats, f32[512,128]{1,0:T(8,128)S(1)} %get-tuple-element.17.worst), custom_call_target="tpu_custom_call" | custom-call | tf_op jit(solution)/shard_map/finish/pallas_call | solution.py:526

commit v6 on v5

--- a/solution.py
+++ b/solution.py
@@ -321,19 +321,17 @@
     def line_gather(r, copies):
         all_sum(r, copies)
         part = hist_out.at[r, mine]
-        back = [send(part, part, fs.at[r, 0], fr.at[r, 0], pair_of(mz))]
+        back = []
         for d in range(1, line):
             t = lax.rem(mz + d, line)
             back.append(send(part, part, gs.at[r, d], gr.at[r, d], line_of(t)))
         return back
 
     def forward(r, back):
-        ends = [back[0]]
-        for d in range(1, line):
-            back[d].wait_recv()
-            part = hist_out.at[r, mx * line + lax.rem(mz + line - d, line)]
-            ends.append(send(part, part, fs.at[r, d], fr.at[r, d], pair_of(mz)))
-        return back[1:], ends
+        for copy in back:
+            copy.wait_recv()
+        part = hist_out.at[r, pl.ds(mx * line, line)]
+        return back, [send(part, part, fs.at[r], fr.at[r], pair_of(mz))]
 
     pltpu.matmul_pop(accs[0])
     pltpu.matmul_pop(accs[1])
@@ -506,7 +504,8 @@
             pltpu.VMEM((3 * combos, LANES), f32),
             pltpu.VMEM((n, 3 * combos, LANES), f32),
         ]
-        + [dma((combos, n))] * 6
+        + [dma((combos, n))] * 4
+        + [dma((combos,))] * 2
         + [dma((n,))] * 2
         + [dma((nc,))] * 4,
         compiler_params=pltpu.CompilerParams(

time: 37.3 us -> 36.7 us (0.984)
  Pallas kernels: 36.4 us -> 35.9 us
    pallas_call x1, Pallas kernels: 35.5 us -> 34.9 us  [on_device(): pl.pallas_call(functools.partial(report, n, nc, GROUPS * bins / endpoints...]
where the time goes in v6:
time: 36.7 us; the launch traced here: 36.6 us
  Pallas kernels  35.9 us (98%)
  between operations  0.64 us (2%)
    pallas_call x1, Pallas kernels, on_device(): pl.pallas_call(functools.partial(report, n, nc, GROUPS * bins / endpoints...  34.9 us
    pallas_call x1, Pallas kernels, on_device(): pl.pallas_call(functools.partial(finish_kernel, endpoints), out_shape=(ja...  0.99 us

profile of v6, /device:TPU:0, one launch (start us, length us, event | category | flops | bytes accessed | tf_op | source)
XLA Modules:
  0.0 36.6 jit_solution(6696281546003845522)
XLA Ops:
  0.6 34.9 %report.1 = (f32[4,8,8,512]{3,2,1,0:T(8,128)S(1)}, f32[12,128]{1,0:T(8,128)S(1)}, f32[512,128]{1,0:T(8,128)S(1)}) custom-call(f32[512,128]{1,0:T(8,128)} %bitcast.26, f32[512,128]{1,0:T(8,128)} %bitcast.27, f32[512,128]{1,0:T(8,128)} %bitcast.28, f32[512,128]{1,0:T(8,128)} %bitcast.29, s32[256,128]{1,0:T(8,128)} %bitcast.30, s32[4,128]{1,0:T(4,128)} %bitcast.31), custom_call_target="tpu_custom_call" | custom-call | tf_op jit(solution)/shard_map/report/pallas_call | solution.py:480
  35.6 1.0 %finish.1 = (f32[64,2,2,512]{3,2,1,0:T(2,128)}, f32[2,2,64]{2,1,0:T(2,128)}, f32[1,64]{1,0:T(1,128)}, f32[2,2]{1,0:T(2,128)}, f32[2,2]{1,0:T(2,128)}, /*index=5*/f32[2,32768]{1,0:T(2,128)}) custom-call(f32[4,64,512]{2,1,0:T(8,128)S(1)} %bitcast.25, f32[12,128]{1,0:T(8,128)S(1)} %get-tuple-element.16.stats, f32[512,128]{1,0:T(8,128)S(1)} %get-tuple-element.17.worst), custom_call_target="tpu_custom_call" | custom-call | tf_op jit(solution)/shard_map/finish/pallas_call | solution.py:525

commit v7 on v6

--- a/solution.py
+++ b/solution.py
@@ -450,9 +450,9 @@
         plan[r, 2] = [("all", r)]
         gather = [("line_gather", r)] if r < last else [("all_gather", r)]
         if r < last - 1:
-            plan[r + 2, 0] = gather
+            plan[r + 2, 1] = gather
             if r > 0:
-                plan[r + 2, 0].append(("forward", r - 1))
+                plan[r + 2, 1].append(("forward", r - 1))
         else:
             if r == last and last > 1:
                 plan["end"].append(("forward", last - 2))

time: 36.7 us -> 36.7 us (level)
  no operation moved by 1% of the time
where the time goes in v7:
time: 36.7 us; the launch traced here: 36.6 us
  Pallas kernels  35.9 us (98%)
  between operations  0.64 us (2%)
    pallas_call x1, Pallas kernels, on_device(): pl.pallas_call(functools.partial(report, n, nc, GROUPS * bins / endpoints...  34.9 us
    pallas_call x1, Pallas kernels, on_device(): pl.pallas_call(functools.partial(finish_kernel, endpoints), out_shape=(ja...  0.99 us

profile of v7, /device:TPU:0, one launch (start us, length us, event | category | flops | bytes accessed | tf_op | source)
XLA Modules:
  0.0 36.6 jit_solution(15263981111642232747)
XLA Ops:
  0.6 34.9 %report.1 = (f32[4,8,8,512]{3,2,1,0:T(8,128)S(1)}, f32[12,128]{1,0:T(8,128)S(1)}, f32[512,128]{1,0:T(8,128)S(1)}) custom-call(f32[512,128]{1,0:T(8,128)} %bitcast.26, f32[512,128]{1,0:T(8,128)} %bitcast.27, f32[512,128]{1,0:T(8,128)} %bitcast.28, f32[512,128]{1,0:T(8,128)} %bitcast.29, s32[256,128]{1,0:T(8,128)} %bitcast.30, s32[4,128]{1,0:T(4,128)} %bitcast.31), custom_call_target="tpu_custom_call" | custom-call | tf_op jit(solution)/shard_map/report/pallas_call | solution.py:480
  35.6 1.0 %finish.1 = (f32[64,2,2,512]{3,2,1,0:T(2,128)}, f32[2,2,64]{2,1,0:T(2,128)}, f32[1,64]{1,0:T(1,128)}, f32[2,2]{1,0:T(2,128)}, f32[2,2]{1,0:T(2,128)}, /*index=5*/f32[2,32768]{1,0:T(2,128)}) custom-call(f32[4,64,512]{2,1,0:T(8,128)S(1)} %bitcast.25, f32[12,128]{1,0:T(8,128)S(1)} %get-tuple-element.16.stats, f32[512,128]{1,0:T(8,128)S(1)} %get-tuple-element.17.worst), custom_call_target="tpu_custom_call" | custom-call | tf_op jit(solution)/shard_map/finish/pallas_call | solution.py:525
